TPU v7x, 256 devices: a whole 4x4x8 slice. The times are simulated.
256 devices in a mesh: ctx: 64 (over z, x_hi, y), tp: 4 (over x_lo, core).
Axes of the slice: x: 4 (x_hi: 2, x_lo: 2; x = x_hi * 2 + x_lo), y: 4, z: 8, core: 2. Of those that a mesh axis runs over, the one named last changes fastest.
Arguments:
- queries: bfloat16 [32768, 4096], P('ctx', 'tp'), may hold values from -22 to 22
- keys: bfloat16 [32768, 512], P('ctx', 'tp'), may hold values from -22 to 22
- values: bfloat16 [32768, 512], P('ctx', 'tp'), may hold values from -36 to 36
- positions: int32 [3, 32768], P(None, 'ctx'), may hold values from 0 to 32767
- segment_ids: int32 [32768], replicated, may hold values from 0 to 31, never falling along the last dimension, each value on 1 to 2048 neighbouring positions
- out_weight: bfloat16 [4096, 8192], P('tp', 'ctx'), may hold values from -0.09375 to 0.09375
- residual: bfloat16 [32768, 8192], P(('ctx', 'tp')), may hold values from -3 to 3
Outputs:
- layer_out: bfloat16 [32768, 8192], P(('ctx', 'tp'))
Inputs may be any that keep to these rules, and one draw needn't show every extreme that they name: `segment_ids`: ids never fall along the sequence; each document has 1 to 2048 tokens, and one has exactly 2048.
All inputs are finite; a program needn't handle non-finite values.
Results may differ from a plain program's by a relative error of at most 0.013.
Values may be sent and summed in bfloat16 or wider, within the bound.
A program may use at most 128 MiB of HBM per device.

v0:
```python
import math
import jax
import jax.numpy as jnp
from jax import lax
from jax.sharding import PartitionSpec as P

HD = 128
DOC = 2048
theta_base = 1000000.0


def from_behind(block, axis, distance):
    devices = range(lax.axis_size(axis))
    route = [(i - distance, i) for i in devices if i - distance in devices]
    return lax.ppermute(block, axis, route)


def rotary_tables(positions):
    half_dim = HD // 2
    freq_index = jnp.arange(half_dim)
    inv_freq = theta_base ** (-2.0 * freq_index.astype(jnp.float32) / HD)
    first_end = HD // 8
    second_end = first_end + 3 * HD // 16
    place = positions.astype(jnp.float32)
    chosen = jnp.where(
        freq_index[None, :] < first_end,
        place[0][:, None],
        jnp.where(freq_index[None, :] < second_end, place[1][:, None], place[2][:, None]),
    )
    angle = chosen * inv_freq[None, :]
    return (jnp.cos(angle), jnp.sin(angle))


def rotate(vectors, cosine_table, sine_table):
    half_dim = HD // 2
    lower_half = vectors[..., :half_dim]
    upper_half = vectors[..., half_dim:]
    cos_b = cosine_table[:, None, :]
    sin_b = sine_table[:, None, :]
    return jnp.concatenate(
        [lower_half * cos_b - upper_half * sin_b, upper_half * cos_b + lower_half * sin_b], axis=-1
    )


def on_device(queries, keys, values, positions, segment_ids, out_weight, residual):
    tok_rows = queries.shape[0]
    local_heads = queries.shape[1] // HD
    local_kv = keys.shape[1] // HD
    group_size = local_heads // local_kv
    reach_blocks = (DOC + tok_rows - 2) // tok_rows
    my_start = lax.axis_index("ctx") * tok_rows
    cosine_table, sine_table = rotary_tables(positions)
    rot_q = rotate(
        queries.reshape(tok_rows, local_heads, HD).astype(jnp.float32), cosine_table, sine_table
    ).astype(jnp.bfloat16)
    grouped = rot_q.reshape(tok_rows, local_kv, group_size, HD).transpose(1, 2, 0, 3)
    rot_k = rotate(
        keys.reshape(tok_rows, local_kv, HD).astype(jnp.float32), cosine_table, sine_table
    ).astype(jnp.bfloat16)
    key_flat = rot_k.reshape(tok_rows, local_kv * HD)
    query_index = my_start + jnp.arange(tok_rows, dtype=jnp.int32)
    query_seg = lax.dynamic_slice_in_dim(segment_ids, my_start, tok_rows, 0)
    score_scale = 1.0 / math.sqrt(HD)
    block_rows = math.gcd(tok_rows, 512)
    block_count = tok_rows // block_rows

    def absorb(running, stacked, offset):
        key_blocks = stacked[0].reshape(block_count, block_rows, local_kv, HD)
        value_blocks = stacked[1].reshape(block_count, block_rows, local_kv, HD)

        def advance(block_index, carried):
            key_block = lax.dynamic_index_in_dim(key_blocks, block_index, 0, keepdims=False)
            value_block = lax.dynamic_index_in_dim(value_blocks, block_index, 0, keepdims=False)
            key_first = offset + block_index * block_rows
            key_index = key_first + jnp.arange(block_rows, dtype=jnp.int32)
            key_seg = lax.dynamic_slice_in_dim(
                segment_ids, jnp.maximum(key_first, 0), block_rows, 0
            )
            allowed = (
                (key_index[None, :] <= query_index[:, None])
                & (key_index[None, :] >= 0)
                & (key_seg[None, :] == query_seg[:, None])
            )

            def update(current):
                row_peak, row_sum, weighted = current
                score = (
                    jnp.einsum(
                        "kgtd,nkd->kgtn", grouped, key_block, preferred_element_type=jnp.float32
                    )
                    * score_scale
                )
                score = jnp.where(allowed, score, -1e30)
                new_peak = jnp.maximum(row_peak, jnp.max(score, axis=-1))
                prob = jnp.where(allowed, jnp.exp(score - new_peak[..., None]), 0.0)
                rescale = jnp.exp(row_peak - new_peak)
                row_sum = row_sum * rescale + jnp.sum(prob, axis=-1)
                weighted = weighted * rescale[..., None] + jnp.einsum(
                    "kgtn,nkd->kgtd",
                    prob.astype(jnp.bfloat16),
                    value_block,
                    preferred_element_type=jnp.float32,
                )
                return (new_peak, row_sum, weighted)

            def keep_state(current):
                return current

            return lax.cond(jnp.any(allowed), update, keep_state, carried)

        return lax.fori_loop(0, block_count, advance, running)

    initial = (
        jnp.full((local_kv, group_size, tok_rows), -1e30, jnp.float32),
        jnp.zeros((local_kv, group_size, tok_rows), jnp.float32),
        jnp.zeros((local_kv, group_size, tok_rows, HD), jnp.float32),
    )
    own_pair = jnp.stack([key_flat, values], axis=0)
    state = absorb(initial, own_pair, my_start)

    def next_block(step_index, carried):
        moving, running = carried
        moving = from_behind(moving, "ctx", 1)
        running = absorb(running, moving, my_start - step_index * tok_rows)
        return (moving, running)

    moving, state = lax.fori_loop(1, reach_blocks + 1, next_block, (own_pair, state))
    row_peak, row_sum, weighted = state
    attended = (
        (weighted / row_sum[..., None])
        .transpose(2, 0, 1, 3)
        .reshape(tok_rows, local_heads * HD)
        .astype(jnp.bfloat16)
    )
    partial_sum = jnp.dot(
        attended,
        lax.all_gather(out_weight, "ctx", axis=1, tiled=True),
        preferred_element_type=jnp.float32,
    )
    partial_sum = partial_sum.astype(jnp.bfloat16).astype(jnp.float32)
    shared = lax.psum_scatter(
        partial_sum.astype(jnp.bfloat16), "tp", scatter_dimension=0, tiled=True
    ).astype(jnp.float32)
    return (shared + residual.astype(jnp.float32)).astype(jnp.bfloat16)


def solution(mesh):
    return jax.shard_map(
        on_device,
        mesh=mesh,
        in_specs=(
            P("ctx", "tp"),
            P("ctx", "tp"),
            P("ctx", "tp"),
            P(None, "ctx"),
            P(),
            P("tp", "ctx"),
            P(("ctx", "tp"), None),
        ),
        out_specs=P(("ctx", "tp"), None),
        check_vma=False,
    )
```

profile of v0, /device:TPU:1, one launch (start us, length us, event | category | flops | bytes accessed | tf_op | source)
XLA Modules:
  0.0 394.7 jit_solution(13520080402836505690)
XLA Ops:
  8.0 1.5 copy.12
  14.2 1.5 broadcast_in_dim.135
  15.7 2.2 subtract_convert_fusion.1
  18.0 8.1 %conditional.2 = ((f32[1,8,512]{2,1,0:T(8,128)S(1)}, f32[1,8,512]{2,1,0:T(8,128)S(1)}, f32[1,8,512,128]{3,2,1,0:T(8,128)})) conditional(s32[]{:T(128)} %convert_element_type.95, (f32[1,8,512]{2,1,0:T(8,128)S(1)}, f32[1,8,512]{2,1,0:T(8,128)S(1)}, f32[1,8,512,128]{3,2,1,0:T(8,128)}) %tuple.39, (pred[512,512]{0,1:T(8,128)(4,1)S(1)}, ...), branch_computations={%region_1.2_spmd, %region_2.0_spmd} | conditional | flops 1102065664 | bytes 49021044 | solution.py:109
  18.0 1.5 fusion.2
  19.6 2.0 fusion.4
  21.6 3.1 bitcast_add_fusion
  24.8 1.3 copy-done.1
  26.1 1.0 pad_maximum_fusion
  27.1 47.2 %while.28 = (s32[]{:T(128)}, bf16[2,512,128]{2,1,0:T(8,128)(2,1)S(1)}, f32[1,8,512]{2,1,0:T(8,128)S(1)}, f32[1,8,512]{2,1,0:T(8,128)S(1)}, f32[1,8,512,128]{3,2,...) while((s32[]{:T(128)}, ...), condition=%wide.region_11.12_spmd.clone.clone, body=%wide.region_5.11_spmd.clone.clone.sunk | while | flops 1103378432 | bytes 50349432 | solution.py:127
  27.2 4.0 %collective-permute-start = (bf16[2,512,128]{2,1,0:T(8,128)(2,1)S(1)}, bf16[2,512,128]{2,1,0:T(8,128)(2,1)S(1)}, u32[]{:S(2)}, u32[]{:S(2)}) collective-permute-start(bf16[2,512,128]{2,1,0:T(8,128)(2,1)S(1)} %get-tuple-element.546), channel_id=1, source_target_pairs={{0,4},{4,8},{8,12},{12,16},{16,20},{20,24},{24,28},{28,32},{32,36}... | collective-permute-start | bytes 786440 | tf_op jit(solution)/shard_map/while/body/eval_jaxpr/ppermute | solution.py:15
  32.0 1.1 fusion.49
  33.8 2.9 collective-permute-done
  36.7 11.1 %collective-permute-start = (bf16[2,512,128]{2,1,0:T(8,128)(2,1)S(1)}, bf16[2,512,128]{2,1,0:T(8,128)(2,1)S(1)}, u32[]{:S(2)}, u32[]{:S(2)}) collective-permute-start(bf16[2,512,128]{2,1,0:T(8,128)(2,1)S(1)} %get-tuple-element.546), channel_id=1, source_target_pairs={{0,4},{4,8},{8,12},{12,16},{16,20},{20,24},{24,28},{28,32},{32,36}... | collective-permute-start | bytes 786440 | tf_op jit(solution)/shard_map/while/body/eval_jaxpr/ppermute | solution.py:15
  48.6 1.1 fusion.49
  51.1 3.8 collective-permute-start
  55.8 1.1 fusion.49
  58.3 12.8 %collective-permute-start = (bf16[2,512,128]{2,1,0:T(8,128)(2,1)S(1)}, bf16[2,512,128]{2,1,0:T(8,128)(2,1)S(1)}, u32[]{:S(2)}, u32[]{:S(2)}) collective-permute-start(bf16[2,512,128]{2,1,0:T(8,128)(2,1)S(1)} %get-tuple-element.546), channel_id=1, source_target_pairs={{0,4},{4,8},{8,12},{12,16},{16,20},{20,24},{24,28},{28,32},{32,36}... | collective-permute-start | bytes 786440 | tf_op jit(solution)/shard_map/while/body/eval_jaxpr/ppermute | solution.py:15
  71.9 1.1 fusion.49
  74.4 1.9 copy.15
  76.6 209.5 %all-gather.2.cloned.1.call-done = bf16[1024,8192]{1,0:T(8,128)(2,1)} async-done(((bf16[1024,128]{1,0:T(8,128)(2,1)}), bf16[1024,8192]{1,0:T(8,128)(2,1)}) %all-gather.2.cloned.1.call-update) | async-done | bytes 16777232 | tf_op jit(solution)/shard_map/all_gather | solution.py:137
  286.1 16.9 %convolution_convert_fusion = bf16[512,8192]{1,0:T(8,128)(2,1)} fusion(bf16[512,1024]{0,1:T(8,128)(2,1)S(1)} %bitcast.79, bf16[1024,8192]{1,0:T(8,128)(2,1)} %all-gather.2.cloned.1.call-done), kind=kOutput, calls=%fused_computation.45 | convolution fusion | flops 8594128896 | bytes 26214400 | tf_op jit(solution)/shard_map/dot_general | solution.py:135
  303.1 81.3 %reduce-scatter.2.cloned.1.call-done = bf16[128,8192]{1,0:T(8,128)(2,1)} async-done(((bf16[512,8192]{1,0:T(8,128)(2,1)}), bf16[128,8192]{1,0:T(8,128)(2,1)}) %reduce-scatter.2.cloned.1.call-update) | async-done | bytes 2097168 | tf_op jit(solution)/shard_map/reduce_scatter | solution.py:141
  384.4 3.4 add_convert_fusion
  (76 shorter events, 11.0 us)
Async XLA Ops:
  6.5 9.1 %copy-start.5 = (bf16[512,128]{1,0:T(8,128)(2,1)S(1)}, bf16[512,128]{1,0:T(8,128)(2,1)}, u32[]{:S(2)}) copy-start(bf16[512,128]{1,0:T(8,128)(2,1)} %param.14) | copy-start | bytes 393220
  6.5 279.6 %all-gather.2.cloned.1.call-start = ((), (), s32[]{:S(2)}) async-start(), calls=%async_computation.1 | async-start | bytes 17039360 | tf_op jit(solution)/shard_map/all_gather | solution.py:137
  7.3 377.1 %reduce-scatter.2.cloned.1.call-start = ((), (), s32[]{:S(2)}) async-start(), calls=%async_computation.2 | async-start | bytes 10485760 | tf_op jit(solution)/shard_map/reduce_scatter | solution.py:141
  10.7 2.3 copy-start.7
  12.3 0.7 copy-start.12
  12.4 0.7 copy-start.13
  12.4 0.7 copy-start.14
  12.4 0.6 copy-start.11
  12.4 1.7 copy-start.9
  12.4 1.7 copy-start.10
  18.0 9.2 %copy-start.8 = (s32[512]{0:T(512)S(1)}, s32[512]{0:T(512)}, u32[]{:S(2)}) copy-start(s32[512]{0:T(512)} %copy-done.7) | copy-start | bytes 6148
  18.0 3.6 copy-start
  18.0 3.6 copy-start.6
  24.8 1.3 copy-start.1
  27.2 9.5 %collective-permute-start = (bf16[2,512,128]{2,1,0:T(8,128)(2,1)S(1)}, bf16[2,512,128]{2,1,0:T(8,128)(2,1)S(1)}, u32[]{:S(2)}, u32[]{:S(2)}) collective-permute-start(bf16[2,512,128]{2,1,0:T(8,128)(2,1)S(1)} %get-tuple-element.546), channel_id=1, source_target_pairs={{0,4},{4,8},{8,12},{12,16},{16,20},{20,24},{24,28},{28,32},{32,36}... | collective-permute-start | bytes 786440 | tf_op jit(solution)/shard_map/while/body/eval_jaxpr/ppermute | solution.py:15
  36.7 14.3 %collective-permute-start = (bf16[2,512,128]{2,1,0:T(8,128)(2,1)S(1)}, bf16[2,512,128]{2,1,0:T(8,128)(2,1)S(1)}, u32[]{:S(2)}, u32[]{:S(2)}) collective-permute-start(bf16[2,512,128]{2,1,0:T(8,128)(2,1)S(1)} %get-tuple-element.546), channel_id=1, source_target_pairs={{0,4},{4,8},{8,12},{12,16},{16,20},{20,24},{24,28},{28,32},{32,36}... | collective-permute-start | bytes 786440 | tf_op jit(solution)/shard_map/while/body/eval_jaxpr/ppermute | solution.py:15
  51.1 7.1 %collective-permute-start = (bf16[2,512,128]{2,1,0:T(8,128)(2,1)S(1)}, bf16[2,512,128]{2,1,0:T(8,128)(2,1)S(1)}, u32[]{:S(2)}, u32[]{:S(2)}) collective-permute-start(bf16[2,512,128]{2,1,0:T(8,128)(2,1)S(1)} %get-tuple-element.546), channel_id=1, source_target_pairs={{0,4},{4,8},{8,12},{12,16},{16,20},{20,24},{24,28},{28,32},{32,36}... | collective-permute-start | bytes 786440 | tf_op jit(solution)/shard_map/while/body/eval_jaxpr/ppermute | solution.py:15
  58.3 16.1 %collective-permute-start = (bf16[2,512,128]{2,1,0:T(8,128)(2,1)S(1)}, bf16[2,512,128]{2,1,0:T(8,128)(2,1)S(1)}, u32[]{:S(2)}, u32[]{:S(2)}) collective-permute-start(bf16[2,512,128]{2,1,0:T(8,128)(2,1)S(1)} %get-tuple-element.546), channel_id=1, source_target_pairs={{0,4},{4,8},{8,12},{12,16},{16,20},{20,24},{24,28},{28,32},{32,36}... | collective-permute-start | bytes 786440 | tf_op jit(solution)/shard_map/while/body/eval_jaxpr/ppermute | solution.py:15
  303.1 81.4 %copy-start.4 = (bf16[128,8192]{1,0:T(8,128)(2,1)S(1)}, bf16[128,8192]{1,0:T(8,128)(2,1)}, u32[]{:S(2)}) copy-start(bf16[128,8192]{1,0:T(8,128)(2,1)} %param.19) | copy-start | bytes 6291460
Sparse Core Ops, SparseCore 0:
  10.7 275.3 all-gather.1
  303.2 81.1 reduce-scatter.1
where the time goes:
time: 395 us
  waiting for transfers between devices  296 us (75%)
  starting transfers between devices  31.8 us (8%)
  matrix products  21.6 us (5%)
  other arithmetic  17.3 us (4%)
  between operations  14.3 us (4%)
  local copies, waits for them, and re-layouts  10.1 us (3%)
    all_gather x1, waiting for transfers between devices, on_device(): lax.all_gather(out_weight, 'ctx', axis=1, tiled=True)  209 us
    reduce_scatter x1, waiting for transfers between devices, on_device(): lax.psum_scatter(partial_sum.astype(jnp.bfloat16), 'tp', scatter_dimensio...  81.3 us
    ppermute x4, starting transfers between devices, from_behind(): return lax.ppermute(block, axis, route)  31.7 us
    dot_general x1, matrix products, on_device(): jnp.dot(attended, lax.all_gather(out_weight, 'ctx', axis=1, tiled=True),...  16.9 us
  transfers between devices with their start and end apart: 6, of which 6 were waited for; matrix products, arithmetic and copies ran while one was open for 7% of the time, Pallas kernels for 0%

commit v1 on v0

--- a/solution.py
+++ b/solution.py
@@ -132,10 +132,11 @@
         .reshape(tok_rows, local_heads * HD)
         .astype(jnp.bfloat16)
     )
+    register_core = lambda on_dim, work_x: jnp.concatenate(
+        jax.lax.all_gather(work_x, "ctx"), axis=on_dim
+    )
     partial_sum = jnp.dot(
-        attended,
-        lax.all_gather(out_weight, "ctx", axis=1, tiled=True),
-        preferred_element_type=jnp.float32,
+        attended, register_core(1, work_x=out_weight), preferred_element_type=jnp.float32
     )
     partial_sum = partial_sum.astype(jnp.bfloat16).astype(jnp.float32)
     shared = lax.psum_scatter(

time: 395 us -> 376 us (0.952)
  waiting for transfers between devices: 296 us -> 240 us
  local copies, waits for them, and re-layouts: 10.1 us -> 31.2 us
  matrix products: 21.6 us -> 34.4 us
  starting transfers between devices: 31.8 us -> 36 us
    all_gather x1, waiting for transfers between devices: 209 us -> 148 us  [on_device(): jax.lax.all_gather(work_x, 'ctx')]
    reshape x0 -> x1, local copies, waits for them, and re-layouts: none -> 22.4 us  [on_device(): jnp.concatenate(jax.lax.all_gather(work_x, 'ctx'), axis=on_dim)]
    dot_general x1, matrix products: 16.9 us -> 29.8 us  [on_device(): jnp.dot(attended, register_core(1, work_x=out_weight), preferred_element_...]
    ppermute x4, waiting for transfers between devices: 4.86 us -> 11.2 us  [from_behind(): return lax.ppermute(block, axis, route)]
    ppermute x4, starting transfers between devices: 31.7 us -> 35.9 us  [from_behind(): return lax.ppermute(block, axis, route)]
where the time goes in v1:
time: 376 us; the launch traced here: 375 us
  waiting for transfers between devices  240 us (64%)
  starting transfers between devices  36 us (10%)
  matrix products  34.4 us (9%)
  local copies, waits for them, and re-layouts  31.2 us (8%)
  other arithmetic  16.4 us (4%)
  between operations  14.2 us (4%)
    all_gather x1, waiting for transfers between devices, on_device(): jax.lax.all_gather(work_x, 'ctx')  148 us
    reduce_scatter x1, waiting for transfers between devices, on_device(): lax.psum_scatter(partial_sum.astype(jnp.bfloat16), 'tp', scatter_dimensio...  79.5 us
    ppermute x4, starting transfers between devices, from_behind(): return lax.ppermute(block, axis, route)  35.9 us
    dot_general x1, matrix products, on_device(): jnp.dot(attended, register_core(1, work_x=out_weight), preferred_element_...  29.8 us
    reshape x1, local copies, waits for them, and re-layouts, on_device(): jnp.concatenate(jax.lax.all_gather(work_x, 'ctx'), axis=on_dim)  22.4 us
    ppermute x4, waiting for transfers between devices, from_behind(): return lax.ppermute(block, axis, route)  11.2 us
  transfers between devices with their start and end apart: 6, of which 6 were waited for; matrix products, arithmetic and copies ran while one was open for 7% of the time, Pallas kernels for 0%

profile of v1, /device:TPU:1, one launch (start us, length us, event | category | flops | bytes accessed | tf_op | source)
XLA Modules:
  0.0 375.2 jit_solution(8102281250525010199)
XLA Ops:
  10.5 1.5 copy.18
  14.1 1.5 broadcast_in_dim.135
  15.6 1.4 subtract_convert_fusion.1
  17.2 7.0 %conditional.2 = ((f32[1,8,512]{2,1,0:T(8,128)S(1)}, f32[1,8,512]{2,1,0:T(8,128)S(1)}, f32[1,8,512,128]{3,2,1,0:T(8,128)})) conditional(s32[]{:T(128)} %convert_element_type.95, (f32[1,8,512]{2,1,0:T(8,128)S(1)}, f32[1,8,512]{2,1,0:T(8,128)S(1)}, f32[1,8,512,128]{3,2,1,0:T(8,128)}) %tuple.39, (pred[512,512]{0,1:T(8,128)(4,1)S(1)}, ...), branch_computations={%region_1.2_spmd, %region_2.0_spmd} | conditional | flops 1102065664 | bytes 48496728 | solution.py:109
  17.2 1.5 fusion.2
  18.8 3.1 bitcast_add_fusion
  21.9 2.0 fusion.4
  24.3 57.3 %while.28 = (s32[]{:T(128)}, bf16[2,512,128]{2,1,0:T(8,128)(2,1)S(1)}, f32[1,8,512]{2,1,0:T(8,128)S(1)}, f32[1,8,512]{2,1,0:T(8,128)S(1)}, f32[1,8,512,128]{3,2,...) while((s32[]{:T(128)}, ...), condition=%wide.region_11.12_spmd.clone.clone, body=%wide.region_5.11_spmd.clone.clone.sunk | while | flops 1103378432 | bytes 50349432 | solution.py:127
  24.3 4.0 %collective-permute-start = (bf16[2,512,128]{2,1,0:T(8,128)(2,1)S(1)}, bf16[2,512,128]{2,1,0:T(8,128)(2,1)S(1)}, u32[]{:S(2)}, u32[]{:S(2)}) collective-permute-start(bf16[2,512,128]{2,1,0:T(8,128)(2,1)S(1)} %get-tuple-element.562), channel_id=1, source_target_pairs={{0,4},{4,8},{8,12},{12,16},{16,20},{20,24},{24,28},{28,32},{32,36}... | collective-permute-start | bytes 786440 | tf_op jit(solution)/shard_map/while/body/eval_jaxpr/ppermute | solution.py:15
  29.2 1.0 fusion.49
  30.9 4.7 %collective-permute-done = bf16[2,512,128]{2,1,0:T(8,128)(2,1)S(1)} collective-permute-done((bf16[2,512,128]{2,1,0:T(8,128)(2,1)S(1)}, bf16[2,512,128]{2,1,0:T(8,128)(2,1)S(1)}, u32[]{:S(2)}, u32[]{:S(2)}) %collective-permute-start) | collective-permute-done | bytes 262176 | tf_op jit(solution)/shard_map/while/body/eval_jaxpr/ppermute | solution.py:15
  35.6 12.3 %collective-permute-start = (bf16[2,512,128]{2,1,0:T(8,128)(2,1)S(1)}, bf16[2,512,128]{2,1,0:T(8,128)(2,1)S(1)}, u32[]{:S(2)}, u32[]{:S(2)}) collective-permute-start(bf16[2,512,128]{2,1,0:T(8,128)(2,1)S(1)} %get-tuple-element.562), channel_id=1, source_target_pairs={{0,4},{4,8},{8,12},{12,16},{16,20},{20,24},{24,28},{28,32},{32,36}... | collective-permute-start | bytes 786440 | tf_op jit(solution)/shard_map/while/body/eval_jaxpr/ppermute | solution.py:15
  50.4 2.3 collective-permute-done
  52.7 4.2 %collective-permute-start = (bf16[2,512,128]{2,1,0:T(8,128)(2,1)S(1)}, bf16[2,512,128]{2,1,0:T(8,128)(2,1)S(1)}, u32[]{:S(2)}, u32[]{:S(2)}) collective-permute-start(bf16[2,512,128]{2,1,0:T(8,128)(2,1)S(1)} %get-tuple-element.562), channel_id=1, source_target_pairs={{0,4},{4,8},{8,12},{12,16},{16,20},{20,24},{24,28},{28,32},{32,36}... | collective-permute-start | bytes 786440 | tf_op jit(solution)/shard_map/while/body/eval_jaxpr/ppermute | solution.py:15
  59.4 1.5 collective-permute-done
  61.0 15.4 %collective-permute-start = (bf16[2,512,128]{2,1,0:T(8,128)(2,1)S(1)}, bf16[2,512,128]{2,1,0:T(8,128)(2,1)S(1)}, u32[]{:S(2)}, u32[]{:S(2)}) collective-permute-start(bf16[2,512,128]{2,1,0:T(8,128)(2,1)S(1)} %get-tuple-element.562), channel_id=1, source_target_pairs={{0,4},{4,8},{8,12},{12,16},{16,20},{20,24},{24,28},{28,32},{32,36}... | collective-permute-start | bytes 786440 | tf_op jit(solution)/shard_map/while/body/eval_jaxpr/ppermute | solution.py:15
  78.9 2.7 collective-permute-done
  81.6 1.9 copy.21
  83.6 1.2 divide_convert_fusion
  84.8 148.5 %all-gather.3.cloned.1.call-done = bf16[65536,128]{1,0:T(8,128)(2,1)} async-done(((bf16[1024,128]{1,0:T(8,128)(2,1)}), bf16[65536,128]{1,0:T(8,128)(2,1)}) %all-gather.3.cloned.1.call-update) | async-done | bytes 16777232 | tf_op jit(solution)/shard_map/all_gather | solution.py:136
  233.3 22.4 %copy.22 = bf16[1024,64,128]{0,2,1:T(8,128)(2,1)} copy(bf16[1024,64,128]{2,0,1:T(8,128)(2,1)} %bitcast.77) | data formatting | bytes 33554432 | tf_op jit(solution)/shard_map/reshape | solution.py:135
  255.7 29.8 %convolution_convert_fusion = bf16[512,8192]{1,0:T(8,128)(2,1)} fusion(bf16[512,1024]{0,1:T(8,128)(2,1)S(1)} %bitcast.85, bf16[1024,8192]{0,1:T(8,128)(2,1)} %bitcast.78), kind=kOutput, calls=%fused_computation.45 | convolution fusion | flops 8594128896 | bytes 26214400 | tf_op jit(solution)/shard_map/dot_general | solution.py:138
  285.5 79.5 %reduce-scatter.2.cloned.1.call-done = bf16[128,8192]{1,0:T(8,128)(2,1)} async-done(((bf16[512,8192]{1,0:T(8,128)(2,1)}), bf16[128,8192]{1,0:T(8,128)(2,1)}) %reduce-scatter.2.cloned.1.call-update) | async-done | bytes 2097168 | tf_op jit(solution)/shard_map/reduce_scatter | solution.py:142
  365.0 3.4 add_convert_fusion
  (63 shorter events, 12.0 us)
Async XLA Ops:
  6.5 9.1 %copy-start.6 = (bf16[512,128]{1,0:T(8,128)(2,1)S(1)}, bf16[512,128]{1,0:T(8,128)(2,1)}, u32[]{:S(2)}) copy-start(bf16[512,128]{1,0:T(8,128)(2,1)} %param.14) | copy-start | bytes 393220
  6.5 226.8 %all-gather.3.cloned.1.call-start = ((), (), s32[]{:S(2)}) async-start(), calls=%async_computation.2 | async-start | bytes 17039360 | tf_op jit(solution)/shard_map/all_gather | solution.py:136
  7.3 357.7 %reduce-scatter.2.cloned.1.call-start = ((), (), s32[]{:S(2)}) async-start(), calls=%async_computation.1 | async-start | bytes 10485760 | tf_op jit(solution)/shard_map/reduce_scatter | solution.py:142
  10.5 6.6 %copy-start.7 = (bf16[512,128]{1,0:T(8,128)(2,1)S(1)}, bf16[512,128]{1,0:T(8,128)(2,1)}, u32[]{:S(2)}) copy-start(bf16[512,128]{1,0:T(8,128)(2,1)} %param.15) | copy-start | bytes 393220
  17.2 1.6 copy-start
  21.9 2.1 copy-start.1
  24.3 11.2 %collective-permute-start = (bf16[2,512,128]{2,1,0:T(8,128)(2,1)S(1)}, bf16[2,512,128]{2,1,0:T(8,128)(2,1)S(1)}, u32[]{:S(2)}, u32[]{:S(2)}) collective-permute-start(bf16[2,512,128]{2,1,0:T(8,128)(2,1)S(1)} %get-tuple-element.562), channel_id=1, source_target_pairs={{0,4},{4,8},{8,12},{12,16},{16,20},{20,24},{24,28},{28,32},{32,36}... | collective-permute-start | bytes 786440 | tf_op jit(solution)/shard_map/while/body/eval_jaxpr/ppermute | solution.py:15
  35.6 17.1 %collective-permute-start = (bf16[2,512,128]{2,1,0:T(8,128)(2,1)S(1)}, bf16[2,512,128]{2,1,0:T(8,128)(2,1)S(1)}, u32[]{:S(2)}, u32[]{:S(2)}) collective-permute-start(bf16[2,512,128]{2,1,0:T(8,128)(2,1)S(1)} %get-tuple-element.562), channel_id=1, source_target_pairs={{0,4},{4,8},{8,12},{12,16},{16,20},{20,24},{24,28},{28,32},{32,36}... | collective-permute-start | bytes 786440 | tf_op jit(solution)/shard_map/while/body/eval_jaxpr/ppermute | solution.py:15
  52.7 8.2 %collective-permute-start = (bf16[2,512,128]{2,1,0:T(8,128)(2,1)S(1)}, bf16[2,512,128]{2,1,0:T(8,128)(2,1)S(1)}, u32[]{:S(2)}, u32[]{:S(2)}) collective-permute-start(bf16[2,512,128]{2,1,0:T(8,128)(2,1)S(1)} %get-tuple-element.562), channel_id=1, source_target_pairs={{0,4},{4,8},{8,12},{12,16},{16,20},{20,24},{24,28},{28,32},{32,36}... | collective-permute-start | bytes 786440 | tf_op jit(solution)/shard_map/while/body/eval_jaxpr/ppermute | solution.py:15
  61.0 20.6 %collective-permute-start = (bf16[2,512,128]{2,1,0:T(8,128)(2,1)S(1)}, bf16[2,512,128]{2,1,0:T(8,128)(2,1)S(1)}, u32[]{:S(2)}, u32[]{:S(2)}) collective-permute-start(bf16[2,512,128]{2,1,0:T(8,128)(2,1)S(1)} %get-tuple-element.562), channel_id=1, source_target_pairs={{0,4},{4,8},{8,12},{12,16},{16,20},{20,24},{24,28},{28,32},{32,36}... | collective-permute-start | bytes 786440 | tf_op jit(solution)/shard_map/while/body/eval_jaxpr/ppermute | solution.py:15
  233.3 22.4 %copy-start.5 = (bf16[1,8,512,128]{2,3,1,0:T(8,128)(2,1)S(1)}, bf16[1,8,512,128]{2,3,1,0:T(8,128)(2,1)}, u32[]{:S(2)}) copy-start(bf16[1,8,512,128]{2,3,1,0:T(8,128)(2,1)} %divide_convert_fusion) | copy-start | bytes 3145732
  285.5 79.5 %copy-start.4 = (bf16[128,8192]{1,0:T(8,128)(2,1)S(1)}, bf16[128,8192]{1,0:T(8,128)(2,1)}, u32[]{:S(2)}) copy-start(bf16[128,8192]{1,0:T(8,128)(2,1)} %param.19) | copy-start | bytes 6291460
Sparse Core Ops, SparseCore 0:
  10.8 222.4 all-gather.2
  285.6 79.3 reduce-scatter.1
